TPU v7x, 128 devices: a whole 4x4x4 slice. The times are simulated.
128 devices in a mesh: dp: 8 (over z_hi, x), section: 4 (over y), tensor: 4 (over z_lo, core).
Axes of the slice: x: 4, y: 4, z: 4 (z_hi: 2, z_lo: 2; z = z_hi * 2 + z_lo), core: 2. Of those that a mesh axis runs over, the one named last changes fastest.
Arguments:
- failed_section: int32 [8], P('dp'), may hold values from 0 to 999
- token_ids: int32 [8, 2048], P('dp'), may hold values from 0 to 100001, as said below
- section_outputs: bfloat16 [8, 4, 2048, 2048], P('dp', 'section', None, 'tensor'), may hold values from -11 to 11
- w_query: float32 [4, 2048, 1024], P('section', 'dp', 'tensor'), may hold values from -1 to 1
- w_key: float32 [4, 2048, 1024], P('section', 'dp', 'tensor'), may hold values from -2 to 2
- w_value: float32 [4, 2048, 1024], P('section', 'dp', 'tensor'), may hold values from -0.125 to 0.125
- w_out: float32 [4, 2048, 1024], P('section', 'dp', 'tensor'), may hold values from -0.75 to 0.75
- m_value: float32 [4, 2048, 1024], P('section', 'dp', 'tensor'), may hold values from -3 to 3
- v_value: float32 [4, 2048, 1024], P('section', 'dp', 'tensor'), may hold values from 0.001 to 1
- m_out: float32 [4, 2048, 1024], P('section', 'dp', 'tensor'), may hold values from -3 to 3
- v_out: float32 [4, 2048, 1024], P('section', 'dp', 'tensor'), may hold values from 0.001 to 1
Outputs:
- restored_query: float32 [8, 4, 2048, 1024], P('dp', 'section', None, 'tensor')
- restored_key: float32 [8, 4, 2048, 1024], P('dp', 'section', None, 'tensor')
- restored_value: float32 [8, 4, 2048, 1024], P('dp', 'section', None, 'tensor')
- restored_out: float32 [8, 4, 2048, 1024], P('dp', 'section', None, 'tensor')
- restored_m_value: float32 [8, 4, 2048, 1024], P('dp', 'section', None, 'tensor')
- restored_v_value: float32 [8, 4, 2048, 1024], P('dp', 'section', None, 'tensor')
- restored_m_out: float32 [8, 4, 2048, 1024], P('dp', 'section', None, 'tensor')
- restored_v_out: float32 [8, 4, 2048, 1024], P('dp', 'section', None, 'tensor')
- attn_update: bfloat16 [8, 4, 2048, 2048], P('dp', 'section', None, 'tensor')
Inputs may be any that keep to these rules, and one draw needn't show every extreme that they name: `token_ids`: token ids of each replica's micro-batch; the id 100001 ends a document, the others are ordinary tokens below 100000.
All inputs are finite; a program needn't handle non-finite values.
Results may differ from a plain program's by a relative error of at most 0.0087.
Values may be sent and summed in bfloat16 or wider, within the bound.
A program may use at most 128 MiB of HBM per device.

v0:
```python
import math
import jax
import jax.numpy as jnp
from jax import lax
from jax.sharding import PartitionSpec as P

HD = 128
end_token = 100001
mask_fill = -1e30


def sent_together(arrays, axis, dim, along):
    ends, at = ([], 0)
    for a in arrays[:-1]:
        at += a.shape[along]
        ends.append(at)
    both = jnp.concatenate(arrays, axis=along)
    return tuple(jnp.split(lax.all_gather(both, axis, axis=dim, tiled=True), ends, axis=along))


def passed_along(array, axis, by):
    count = lax.axis_size(axis)
    return lax.ppermute(array, axis, [(i, (i + by) % count) for i in range(count)])


def document_ids(token_row):
    doc_ends = (token_row == end_token).astype(jnp.int32)
    return jnp.cumsum(doc_ends) - doc_ends


def attend(queries, key_vals, value_vals, token_row):
    token_count = queries.shape[0]
    heads_local = queries.shape[1] // HD
    block_rows = min(512, token_count)
    document = document_ids(token_row)
    positions = jnp.arange(token_count, dtype=jnp.int32)
    key_heads = key_vals.reshape(token_count, heads_local, HD)
    value_heads = value_vals.reshape(token_count, heads_local, HD)

    def one_block(block_index):
        first_row = block_index * block_rows
        query_block = lax.dynamic_slice_in_dim(queries, first_row, block_rows, 0).reshape(
            block_rows, heads_local, HD
        )
        scores = jnp.einsum(
            "qhd,khd->hqk", query_block, key_heads, preferred_element_type=jnp.float32
        ) * (1.0 / math.sqrt(HD))
        query_pos = lax.dynamic_slice_in_dim(positions, first_row, block_rows, 0)
        query_doc = lax.dynamic_slice_in_dim(document, first_row, block_rows, 0)
        allowed = (positions[None, :] <= query_pos[:, None]) & (
            document[None, :] == query_doc[:, None]
        )
        scores = jnp.where(allowed[None], scores, mask_fill)
        highest = jnp.max(scores, axis=2, keepdims=True)
        weights = jnp.exp(scores - highest)
        probs = (weights / jnp.sum(weights, axis=2, keepdims=True)).astype(jnp.bfloat16)
        context = jnp.einsum(
            "hqk,khd->qhd", probs, value_heads, preferred_element_type=jnp.float32
        ).astype(jnp.bfloat16)
        return context.reshape(block_rows, heads_local * HD)

    blocks = lax.map(one_block, jnp.arange(token_count // block_rows, dtype=jnp.int32))
    return blocks.reshape(token_count, heads_local * HD)


def shards(
    failed_section,
    token_ids,
    section_outputs,
    w_query,
    w_key,
    w_value,
    w_out,
    m_value,
    v_value,
    m_out,
    v_out,
):
    section_failed = jnp.remainder(failed_section[0], lax.axis_size("section"))
    replacing = lax.axis_index("section") == section_failed
    masters = tuple(
        (
            part.astype(jnp.float32)
            for part in sent_together(
                (
                    w_query.astype(jnp.bfloat16),
                    w_key.astype(jnp.bfloat16),
                    w_value.astype(jnp.bfloat16),
                    w_out.astype(jnp.bfloat16),
                ),
                "dp",
                1,
                0,
            )
        )
    )
    query_bf = masters[0][0].astype(jnp.bfloat16)
    key_bf = masters[1][0].astype(jnp.bfloat16)
    value_bf = masters[2][0].astype(jnp.bfloat16)
    out_bf = masters[3][0].astype(jnp.bfloat16)
    inner_local = query_bf.shape[1]
    w_joined = jnp.concatenate([query_bf, key_bf, value_bf], axis=1)
    incoming = passed_along(section_outputs, "section", 1)
    projected = jnp.dot(
        lax.all_gather(incoming, "tensor", axis=3, tiled=True)[0, 0],
        w_joined,
        preferred_element_type=jnp.float32,
    )
    queries = projected[:, :inner_local].astype(jnp.bfloat16)
    key_vals = projected[:, inner_local : 2 * inner_local].astype(jnp.bfloat16)
    value_vals = projected[:, 2 * inner_local :].astype(jnp.bfloat16)
    context = attend(queries, key_vals, value_vals, token_ids[0])
    context_whole = lax.all_gather(context, "tensor", axis=1, tiled=True)
    out_slice = lax.all_to_all(out_bf, "tensor", split_axis=0, concat_axis=1, tiled=True)
    update = lax.dot_general(
        context_whole, out_slice, (((1,), (1,)), ((), ())), preferred_element_type=jnp.float32
    ).astype(jnp.bfloat16)
    moments = tuple(
        (
            part.astype(jnp.float32)
            for part in sent_together(
                (
                    m_value.astype(jnp.bfloat16),
                    v_value.astype(jnp.bfloat16),
                    m_out.astype(jnp.bfloat16),
                    v_out.astype(jnp.bfloat16),
                ),
                "dp",
                1,
                0,
            )
        )
    )

    def placed(gathered):
        return jnp.where(replacing, gathered[None], jnp.zeros_like(gathered[None]))

    update_block = jnp.where(
        replacing, update[None, None], jnp.zeros((1, 1) + update.shape, jnp.bfloat16)
    )
    return (
        placed(masters[0]),
        placed(masters[1]),
        placed(masters[2]),
        placed(masters[3]),
        placed(moments[0]),
        placed(moments[1]),
        placed(moments[2]),
        placed(moments[3]),
        update_block,
    )


def solution(mesh):
    return jax.shard_map(
        shards,
        mesh=mesh,
        in_specs=(
            P("dp"),
            P("dp", None),
            P("dp", "section", None, "tensor"),
            P("section", "dp", "tensor"),
            P("section", "dp", "tensor"),
            P("section", "dp", "tensor"),
            P("section", "dp", "tensor"),
            P("section", "dp", "tensor"),
            P("section", "dp", "tensor"),
            P("section", "dp", "tensor"),
            P("section", "dp", "tensor"),
        ),
        out_specs=(
            P("dp", "section", None, "tensor"),
            P("dp", "section", None, "tensor"),
            P("dp", "section", None, "tensor"),
            P("dp", "section", None, "tensor"),
            P("dp", "section", None, "tensor"),
            P("dp", "section", None, "tensor"),
            P("dp", "section", None, "tensor"),
            P("dp", "section", None, "tensor"),
            P("dp", "section", None, "tensor"),
        ),
        check_vma=False,
    )
```

profile of v0, /device:TPU:1, one launch (start us, length us, event | category | flops | bytes accessed | tf_op | source)
XLA Modules:
  0.0 302.3 jit_solution(5347417715151155394)
XLA Ops:
  7.3 1.0 convert_element_type.92
  8.3 1.0 convert_element_type.93
  9.3 1.0 convert_element_type.94
  10.2 1.0 convert_element_type.95
  11.2 0.9 pad_maximum_fusion
  12.2 2.2 collective-permute-start
  14.3 47.0 %collective-permute-done = bf16[1,1,2048,512]{3,2,1,0:T(8,128)(2,1)S(1)} collective-permute-done((bf16[1,1,2048,512]{3,2,1,0:T(8,128)(2,1)}, bf16[1,1,2048,512]{3,2,1,0:T(8,128)(2,1)S(1)}, u32[]{:S(2)}, u32[]{:S(2)}) %collective-permute-start) | collective-permute-done | bytes 2097184 | tf_op jit(solution)/shard_map/ppermute | solution.py:23
  61.3 1.3 copy-done
  62.9 0.9 pad_maximum_fusion.1
  64.4 21.9 %all-gather.5.cloned.1.call-done = bf16[4,2048,256]{2,1,0:T(8,128)(2,1)} async-done(((bf16[4,256,256]{2,1,0:T(8,128)(2,1)}), bf16[4,2048,256]{2,1,0:T(8,128)(2,1)}) %all-gather.5.cloned.1.call-update) | async-done | bytes 4194320 | tf_op jit(solution)/shard_map/all_gather | solution.py:18
  86.3 3.4 %fusion.30 = (bf16[1,2048,256]{2,1,0:T(8,128)(2,1)}, bf16[2048,256]{1,0:T(8,128)(2,1)S(1)}, bf16[2048,256]{1,0:T(8,128)(2,1)S(1)}, bf16[2048,256]{1,0:T(8,128)(2,1)S(1)}) fusion(bf16[4,2048,256]{2,1,0:T(8,128)(2,1)} %all-gather.5.cloned.1.call-done), kind=kLoop, calls=%fused_computation.46 | loop fusion | bytes 8388608 | tf_op jit(solution)/shard_map/split | solution.py:18
  89.7 79.1 %all-gather.9.cloned.1.call-done = bf16[1,1,2048,2048]{3,2,1,0:T(8,128)(2,1)} async-done(((bf16[1,1,2048,512]{3,2,1,0:T(8,128)(2,1)}), bf16[1,1,2048,2048]{3,2,1,0:T(8,128)(2,1)}) %all-gather.9.cloned.1.call-update) | async-done | bytes 8388624 | tf_op jit(solution)/shard_map/all_gather | solution.py:105
  168.8 9.1 %fusion.21 = bf16[2048,768]{0,1:T(8,128)(2,1)S(1)} fusion(bf16[1,1,2048,2048]{3,2,1,0:T(8,128)(2,1)} %all-gather.9.cloned.1.call-done, bf16[2048,256]{1,0:T(8,128)(2,1)S(1)} %get-tuple-element.120, bf16[2048,256]{1,0:T(8,128)(2,1)S(1)} %get-tuple-element.119, bf16[2048,256]{1,0:T(8,128)(2,1)S(1)} %get-tuple-element.118), kind=kOutput, calls=%fused_computation.24 | convolution fusion | flops 6453460992 | bytes 14680064 | tf_op jit(solution)/shard_map/dot_general | solution.py:104
  178.0 1.2 fusion.31
  179.9 54.7 %while.11 = (s32[]{:T(128)}, bf16[4,512,256]{2,1,0:T(8,128)(2,1)}, s32[2048]{0:T(1024)S(1)}, s32[4]{0:T(128)S(1)}, s32[2048]{0:T(1024)S(1)}, /*index=5*/bf16[204...) while((s32[]{:T(128)}, bf16[4,512,256]{2,1,0:T(8,128)(2,1)}, ...), condition=%wide.region_5.6_spmd.clone, body=%wide.region_2.5_spmd.clone.sunk | while | flops 1089603584 | bytes 23106236 | solution.py:62
  181.3 0.9 compare_and_fusion.2
  182.3 5.2 %fusion.47 = (f32[2,512]{1,0:T(2,128)S(1)}, f32[2,512,2048]{2,1,0:T(8,128)}) fusion(pred[512,2048]{1,0:T(8,128)(4,1)S(1)} %compare_and_fusion.2, bf16[512,2,128]{0,2,1:T(8,128)(2,1)S(1)} %bitcast.71, bf16[2048,2,128]{2,0,1:T(8,128)(2,1)S(1)} %get-tuple-element.215), kind=kOutput, calls=%fused_computation.45.clone.1 | convolution fusion | flops 545261568 | bytes 10752000 | tf_op jit(solution)/shard_map/while/body/eval_jaxpr/sub | solution.py:55
  187.5 5.2 %fusion.48 = bf16[2,512,128]{1,2,0:T(8,128)(2,1)S(1)} fusion(bf16[2048,2,128]{0,2,1:T(8,128)(2,1)} %get-tuple-element.216, f32[2,512,2048]{2,1,0:T(8,128)} %get-tuple-element.183, f32[2,512]{1,0:T(2,128)S(1)} %get-tuple-element.184), kind=kOutput, calls=%fused_computation.10.clone.1 | convolution fusion | flops 541196288 | bytes 9703424 | tf_op jit(solution)/shard_map/while/body/eval_jaxpr/hqk,khd->qhd/dot_general | solution.py:57
  195.0 0.9 compare_and_fusion.2
  196.0 5.2 %fusion.47 = (f32[2,512]{1,0:T(2,128)S(1)}, f32[2,512,2048]{2,1,0:T(8,128)}) fusion(pred[512,2048]{1,0:T(8,128)(4,1)S(1)} %compare_and_fusion.2, bf16[512,2,128]{0,2,1:T(8,128)(2,1)S(1)} %bitcast.71, bf16[2048,2,128]{2,0,1:T(8,128)(2,1)S(1)} %get-tuple-element.215), kind=kOutput, calls=%fused_computation.45.clone.1 | convolution fusion | flops 545261568 | bytes 10752000 | tf_op jit(solution)/shard_map/while/body/eval_jaxpr/sub | solution.py:55
  201.2 5.2 %fusion.48 = bf16[2,512,128]{1,2,0:T(8,128)(2,1)S(1)} fusion(bf16[2048,2,128]{0,2,1:T(8,128)(2,1)} %get-tuple-element.216, f32[2,512,2048]{2,1,0:T(8,128)} %get-tuple-element.183, f32[2,512]{1,0:T(2,128)S(1)} %get-tuple-element.184), kind=kOutput, calls=%fused_computation.10.clone.1 | convolution fusion | flops 541196288 | bytes 9703424 | tf_op jit(solution)/shard_map/while/body/eval_jaxpr/hqk,khd->qhd/dot_general | solution.py:57
  208.7 0.9 compare_and_fusion.2
  209.6 5.2 %fusion.47 = (f32[2,512]{1,0:T(2,128)S(1)}, f32[2,512,2048]{2,1,0:T(8,128)}) fusion(pred[512,2048]{1,0:T(8,128)(4,1)S(1)} %compare_and_fusion.2, bf16[512,2,128]{0,2,1:T(8,128)(2,1)S(1)} %bitcast.71, bf16[2048,2,128]{2,0,1:T(8,128)(2,1)S(1)} %get-tuple-element.215), kind=kOutput, calls=%fused_computation.45.clone.1 | convolution fusion | flops 545261568 | bytes 10752000 | tf_op jit(solution)/shard_map/while/body/eval_jaxpr/sub | solution.py:55
  214.8 5.3 %fusion.48 = bf16[2,512,128]{1,2,0:T(8,128)(2,1)S(1)} fusion(bf16[2048,2,128]{0,2,1:T(8,128)(2,1)} %get-tuple-element.216, f32[2,512,2048]{2,1,0:T(8,128)} %get-tuple-element.183, f32[2,512]{1,0:T(2,128)S(1)} %get-tuple-element.184), kind=kOutput, calls=%fused_computation.10.clone.1 | convolution fusion | flops 541196288 | bytes 9703424 | tf_op jit(solution)/shard_map/while/body/eval_jaxpr/hqk,khd->qhd/dot_general | solution.py:57
  222.4 0.9 compare_and_fusion.2
  223.3 5.2 %fusion.47 = (f32[2,512]{1,0:T(2,128)S(1)}, f32[2,512,2048]{2,1,0:T(8,128)}) fusion(pred[512,2048]{1,0:T(8,128)(4,1)S(1)} %compare_and_fusion.2, bf16[512,2,128]{0,2,1:T(8,128)(2,1)S(1)} %bitcast.71, bf16[2048,2,128]{2,0,1:T(8,128)(2,1)S(1)} %get-tuple-element.215), kind=kOutput, calls=%fused_computation.45.clone.1 | convolution fusion | flops 545261568 | bytes 10752000 | tf_op jit(solution)/shard_map/while/body/eval_jaxpr/sub | solution.py:55
  228.5 5.2 %fusion.48 = bf16[2,512,128]{1,2,0:T(8,128)(2,1)S(1)} fusion(bf16[2048,2,128]{0,2,1:T(8,128)(2,1)} %get-tuple-element.216, f32[2,512,2048]{2,1,0:T(8,128)} %get-tuple-element.183, f32[2,512]{1,0:T(2,128)S(1)} %get-tuple-element.184), kind=kOutput, calls=%fused_computation.10.clone.1 | convolution fusion | flops 541196288 | bytes 9703424 | tf_op jit(solution)/shard_map/while/body/eval_jaxpr/hqk,khd->qhd/dot_general | solution.py:57
  235.3 3.7 %all-to-all-start = ((bf16[4,512,256]{2,1,0:T(8,128)(2,1)}), bf16[4,512,256]{2,1,0:T(8,128)(2,1)S(1)}, u32[]{:S(2)}, u32[]{:S(2)}) async-start(bf16[4,512,256]{2,1,0:T(8,128)(2,1)} %bitcast.20), calls=%async_computation | async-start | bytes 2097152 | tf_op jit(solution)/shard_map/all_to_all | solution.py:114
  239.0 5.7 %select_bitcast_fusion.4 = (f32[1,1,2048,256]{3,2,1,0:T(8,128)}, f32[1,1,2048,256]{3,2,1,0:T(8,128)}, f32[1,1,2048,256]{3,2,1,0:T(8,128)}, f32[1,1,2048,256]{3,2,1,0:T(8,128)}) fusion(pred[]{:T(512)S(6)} %eq.31, bf16[4,2048,256]{2,1,0:T(8,128)(2,1)} %all-gather.5.cloned.1.call-done), kind=kLoop, calls=%fused_computation.32 | loop fusion | flops 4194304 | bytes 12582913 | tf_op jit(solution)/shard_map/jit(_where)/select_n | solution.py:136
  244.7 5.7 %select_bitcast_fusion = (f32[1,1,2048,256]{3,2,1,0:T(8,128)}, f32[1,1,2048,256]{3,2,1,0:T(8,128)}, f32[1,1,2048,256]{3,2,1,0:T(8,128)}, f32[1,1,2048,256]{3,2,1,0:T(8,128)}) fusion(bf16[4,2048,256]{2,1,0:T(8,128)(2,1)} %all-gather.7.cloned.1.call-done, pred[]{:T(512)S(6)} %eq.31), kind=kLoop, calls=%fused_computation.28 | loop fusion | flops 4194304 | bytes 12582913 | tf_op jit(solution)/shard_map/jit(_where)/select_n | solution.py:136
  251.6 38.3 %all-gather.11.cloned.1.call-done = bf16[2048,1024]{1,0:T(8,128)(2,1)} async-done(((bf16[2048,256]{1,0:T(8,128)(2,1)}), bf16[2048,1024]{1,0:T(8,128)(2,1)}) %all-gather.11.cloned.1.call-update) | async-done | bytes 4194320 | tf_op jit(solution)/shard_map/all_gather | solution.py:113
  290.0 5.8 %fusion.27 = bf16[1,1,2048,512]{3,2,1,0:T(8,128)(2,1)} fusion(bf16[2048,1024]{1,0:T(8,128)(2,1)} %all-gather.11.cloned.1.call-done, bf16[512,1024]{0,1:T(8,128)(2,1)S(1)} %bitcast.76, pred[]{:T(512)S(6)} %eq.31), kind=kOutput, calls=%fused_computation.27 | convolution fusion | flops 2149580800 | bytes 7340033 | tf_op jit(solution)/shard_map/dot_general | solution.py:115
  (60 shorter events, 9.4 us)
Async XLA Ops:
  7.2 55.5 %copy-start.1 = (f32[1,256,256]{2,1,0:T(8,128)S(1)}, f32[1,256,256]{2,1,0:T(8,128)}, u32[]{:S(2)}) copy-start(f32[1,256,256]{2,1,0:T(8,128)} %param.20) | copy-start | bytes 786436
  7.2 55.6 %copy-start.2 = (f32[1,256,256]{2,1,0:T(8,128)S(1)}, f32[1,256,256]{2,1,0:T(8,128)}, u32[]{:S(2)}) copy-start(f32[1,256,256]{2,1,0:T(8,128)} %param.21) | copy-start | bytes 786436
  7.2 55.6 %copy-start.3 = (f32[1,256,256]{2,1,0:T(8,128)S(1)}, f32[1,256,256]{2,1,0:T(8,128)}, u32[]{:S(2)}) copy-start(f32[1,256,256]{2,1,0:T(8,128)} %param.22) | copy-start | bytes 786436
  7.2 55.6 %copy-start.4 = (f32[1,256,256]{2,1,0:T(8,128)S(1)}, f32[1,256,256]{2,1,0:T(8,128)}, u32[]{:S(2)}) copy-start(f32[1,256,256]{2,1,0:T(8,128)} %param.23) | copy-start | bytes 786436
  7.2 79.1 %all-gather.5.cloned.1.call-start = ((), (), s32[]{:S(2)}) async-start(), calls=%async_computation.1 | async-start | bytes 4718592 | tf_op jit(solution)/shard_map/all_gather | solution.py:18
  12.1 51.7 %copy-start.5 = (s32[1,2048]{1,0:T(1,128)S(1)}, s32[1,2048]{1,0:T(1,128)}, u32[]{:S(2)}) copy-start(s32[1,2048]{1,0:T(1,128)} %param.14) | copy-start | bytes 24580
  12.1 156.7 %all-gather.9.cloned.1.call-start = ((), (), s32[]{:S(2)}) async-start(), calls=%async_computation.3 | async-start | bytes 10485760 | tf_op jit(solution)/shard_map/all_gather | solution.py:105
  12.2 49.2 %collective-permute-start = (bf16[1,1,2048,512]{3,2,1,0:T(8,128)(2,1)}, bf16[1,1,2048,512]{3,2,1,0:T(8,128)(2,1)S(1)}, u32[]{:S(2)}, u32[]{:S(2)}) collective-permute-start(bf16[1,1,2048,512]{3,2,1,0:T(8,128)(2,1)} %param.15), channel_id=1, source_target_pairs={{0,4},{4,8},{8,12},{12,0},{1,5},{5,9},{9,13},{13,1},{2,6},{6,10},{... | collective-permute-start | bytes 6291464 | tf_op jit(solution)/shard_map/ppermute | solution.py:23
  61.3 1.3 copy-start
  62.7 182.0 %all-gather.7.cloned.1.call-start = ((), (), s32[]{:S(2)}) async-start(), calls=%async_computation.2 | async-start | bytes 4718592 | tf_op jit(solution)/shard_map/all_gather | solution.py:18
  63.7 226.2 %all-gather.11.cloned.1.call-start = ((), (), s32[]{:S(2)}) async-start(), calls=%async_computation.4 | async-start | bytes 5242880 | tf_op jit(solution)/shard_map/all_gather | solution.py:113
  235.3 15.8 %all-to-all-start = ((bf16[4,512,256]{2,1,0:T(8,128)(2,1)}), bf16[4,512,256]{2,1,0:T(8,128)(2,1)S(1)}, u32[]{:S(2)}, u32[]{:S(2)}) async-start(bf16[4,512,256]{2,1,0:T(8,128)(2,1)} %bitcast.20), calls=%async_computation | async-start | bytes 2097152 | tf_op jit(solution)/shard_map/all_to_all | solution.py:114
Sparse Core Ops, SparseCore 0:
  12.2 74.0 all-gather.4
  88.5 80.2 all-gather.8
  171.8 71.3 all-gather.6
  244.7 45.2 all-gather.10
where the time goes:
time: 303 us; the launch traced here: 302 us
  waiting for transfers between devices  187 us (62%)
  matrix products  56.7 us (19%)
  other arithmetic  21.1 us (7%)
  between operations  14.6 us (5%)
  local copies, waits for them, and re-layouts  13.9 us (5%)
  starting transfers between devices  6.04 us (2%)
    all_gather x1, waiting for transfers between devices, shards(): lax.all_gather(incoming, 'tensor', axis=3, tiled=True)[0, 0]  79.1 us
    ppermute x1, waiting for transfers between devices, passed_along(): lax.ppermute(array, axis, [(i, (i + by) % count) for i in range(count)])  47 us
    all_gather x1, waiting for transfers between devices, shards(): context_whole = lax.all_gather(context, 'tensor', axis=1, tiled=True)  38.3 us
    all_gather x2, waiting for transfers between devices, sent_together(): lax.all_gather(both, axis, axis=dim, tiled=True)  21.9 us
    dot_general x4, matrix products, one_block(): jnp.einsum('hqk,khd->qhd', probs, value_heads, preferred_element_type=jnp...  20.9 us
    sub x4, matrix products, one_block(): weights = jnp.exp(scores - highest)  20.8 us
    select_n x2, other arithmetic, placed(): return jnp.where(replacing, gathered[None], jnp.zeros_like(gathered[None]))  11.3 us
    dot_general x1, matrix products, shards(): jnp.dot(lax.all_gather(incoming, 'tensor', axis=3, tiled=True)[0, 0], w_j...  9.14 us
  transfers between devices with their start and end apart: 6, of which 5 were waited for; matrix products, arithmetic and copies ran while one was open for 26% of the time, Pallas kernels for 0%

commit v1 on v0

--- a/solution.py
+++ b/solution.py
@@ -7,6 +7,13 @@
 HD = 128
 end_token = 100001
 mask_fill = -1e30
+
+
+def all_by_exchange(x, axis, dim):
+    size = lax.axis_size(axis)
+    blocks = jnp.stack([x for _ in range(size)])
+    blocks = lax.all_to_all(blocks, axis, split_axis=0, concat_axis=0)
+    return jnp.concatenate(blocks, axis=dim)
 
 
 def sent_together(arrays, axis, dim, along):
@@ -110,7 +117,7 @@
     key_vals = projected[:, inner_local : 2 * inner_local].astype(jnp.bfloat16)
     value_vals = projected[:, 2 * inner_local :].astype(jnp.bfloat16)
     context = attend(queries, key_vals, value_vals, token_ids[0])
-    context_whole = lax.all_gather(context, "tensor", axis=1, tiled=True)
+    context_whole = all_by_exchange(context, "tensor", 1)
     out_slice = lax.all_to_all(out_bf, "tensor", split_axis=0, concat_axis=1, tiled=True)
     update = lax.dot_general(
         context_whole, out_slice, (((1,), (1,)), ((), ())), preferred_element_type=jnp.float32

time: 303 us -> 319 us (1.053)
  matrix products: 56.7 us -> 67.8 us
  starting transfers between devices: 6.04 us -> 13 us
    all_gather x1 -> x0, waiting for transfers between devices: 38.3 us -> none  [shards(): context_whole = lax.all_gather(context, 'tensor', axis=1, tiled=True)]
    all_to_all x0 -> x1, waiting for transfers between devices: none -> 35.3 us  [all_by_exchange(): blocks = lax.all_to_all(blocks, axis, split_axis=0, concat_axis=0)]
    sub x4, matrix products: 20.8 us -> 31.3 us  [one_block(): weights = jnp.exp(scores - highest)]
    all_to_all x0 -> x1, starting transfers between devices: none -> 5.04 us  [all_by_exchange(): blocks = lax.all_to_all(blocks, axis, split_axis=0, concat_axis=0)]
  transfers between devices with their start and end apart: 6 -> 6, of which waited for: 5 -> 4; matrix products, arithmetic and copies ran while one was open for 26% -> 28% of each run, Pallas kernels for 0% -> 0%
where the time goes in v1:
time: 319 us
  waiting for transfers between devices  186 us (58%)
  matrix products  67.8 us (21%)
  other arithmetic  21.1 us (7%)
  between operations  14.6 us (5%)
  local copies, waits for them, and re-layouts  13.8 us (4%)
  starting transfers between devices  13 us (4%)
    all_gather x1, waiting for transfers between devices, shards(): lax.all_gather(incoming, 'tensor', axis=3, tiled=True)[0, 0]  81.5 us
    ppermute x1, waiting for transfers between devices, passed_along(): lax.ppermute(array, axis, [(i, (i + by) % count) for i in range(count)])  47 us
    all_to_all x1, waiting for transfers between devices, all_by_exchange(): blocks = lax.all_to_all(blocks, axis, split_axis=0, concat_axis=0)  35.3 us
    sub x4, matrix products, one_block(): weights = jnp.exp(scores - highest)  31.3 us
    all_gather x2, waiting for transfers between devices, sent_together(): lax.all_gather(both, axis, axis=dim, tiled=True)  21.9 us
    dot_general x4, matrix products, one_block(): jnp.einsum('hqk,khd->qhd', probs, value_heads, preferred_element_type=jnp...  20.9 us
    select_n x2, other arithmetic, placed(): return jnp.where(replacing, gathered[None], jnp.zeros_like(gathered[None]))  11.3 us
    dot_general x1, matrix products, shards(): jnp.dot(lax.all_gather(incoming, 'tensor', axis=3, tiled=True)[0, 0], w_j...  9.45 us
  transfers between devices with their start and end apart: 6, of which 4 were waited for; matrix products, arithmetic and copies ran while one was open for 28% of the time, Pallas kernels for 0%

profile of v1, /device:TPU:1, one launch (start us, length us, event | category | flops | bytes accessed | tf_op | source)
XLA Modules:
  0.0 318.9 jit_solution(13650835602294083294)
XLA Ops:
  7.3 1.0 convert_element_type.92
  8.3 1.0 convert_element_type.93
  9.3 1.0 convert_element_type.94
  10.3 1.0 convert_element_type.95
  12.2 2.2 collective-permute-start
  14.3 47.0 %collective-permute-done = bf16[1,1,2048,512]{3,2,1,0:T(8,128)(2,1)S(1)} collective-permute-done((bf16[1,1,2048,512]{3,2,1,0:T(8,128)(2,1)}, bf16[1,1,2048,512]{3,2,1,0:T(8,128)(2,1)S(1)}, u32[]{:S(2)}, u32[]{:S(2)}) %collective-permute-start) | collective-permute-done | bytes 2097184 | tf_op jit(solution)/shard_map/ppermute | solution.py:30
  61.3 1.3 copy-done
  64.4 21.9 %all-gather.4.cloned.1.call-done = bf16[4,2048,256]{2,1,0:T(8,128)(2,1)} async-done(((bf16[4,256,256]{2,1,0:T(8,128)(2,1)}), bf16[4,2048,256]{2,1,0:T(8,128)(2,1)}) %all-gather.4.cloned.1.call-update) | async-done | bytes 4194320 | tf_op jit(solution)/shard_map/all_gather | solution.py:25
  86.3 3.8 %fusion.39 = (bf16[1,2048,256]{2,1,0:T(8,128)(2,1)}, bf16[2048,256]{1,0:T(8,128)(2,1)S(1)}, bf16[2048,256]{1,0:T(8,128)(2,1)S(1)}, bf16[2048,256]{1,0:T(8,128)(2,1)}) fusion(bf16[4,2048,256]{2,1,0:T(8,128)(2,1)} %all-gather.4.cloned.1.call-done), kind=kLoop, calls=%fused_computation.49 | loop fusion | bytes 8388608 | tf_op jit(solution)/shard_map/split | solution.py:25
  90.1 5.6 %all-to-all-start.1 = ((bf16[4,512,256]{2,1,0:T(8,128)(2,1)}), bf16[4,512,256]{2,1,0:T(8,128)(2,1)}, u32[]{:S(2)}, u32[]{:S(2)}) async-start(bf16[4,512,256]{2,1,0:T(8,128)(2,1)} %bitcast.21), calls=%async_computation.1 | async-start | bytes 2097152 | tf_op jit(solution)/shard_map/all_to_all | solution.py:121
  95.7 81.5 %all-gather.8.cloned.1.call-done = bf16[1,1,2048,2048]{3,2,1,0:T(8,128)(2,1)} async-done(((bf16[1,1,2048,512]{3,2,1,0:T(8,128)(2,1)}), bf16[1,1,2048,2048]{3,2,1,0:T(8,128)(2,1)}) %all-gather.8.cloned.1.call-update) | async-done | bytes 8388624 | tf_op jit(solution)/shard_map/all_gather | solution.py:112
  177.2 9.4 %fusion.23 = bf16[2048,768]{0,1:T(8,128)(2,1)S(1)} fusion(bf16[1,1,2048,2048]{3,2,1,0:T(8,128)(2,1)} %all-gather.8.cloned.1.call-done, bf16[2048,256]{1,0:T(8,128)(2,1)} %get-tuple-element.112, bf16[2048,256]{1,0:T(8,128)(2,1)S(1)} %get-tuple-element.111, bf16[2048,256]{1,0:T(8,128)(2,1)S(1)} %get-tuple-element.110), kind=kOutput, calls=%fused_computation.27 | convolution fusion | flops 6453460992 | bytes 14680064 | tf_op jit(solution)/shard_map/dot_general | solution.py:111
  186.6 1.2 fusion.40
  187.9 1.3 copy.23
  189.2 62.4 %while.11 = (s32[]{:T(128)}, bf16[4,512,256]{2,1,0:T(8,128)(2,1)S(1)}, s32[2048]{0:T(1024)S(1)}, s32[4]{0:T(128)S(1)}, s32[2048]{0:T(1024)S(1)}, /*index=5*/bf16...) while((s32[]{:T(128)}, ...), condition=%wide.region_5.6_spmd.clone, body=%wide.region_2.5_spmd.clone.sunk | while | flops 1089603584 | bytes 23105728 | solution.py:69
  191.5 7.8 %fusion.54 = (f32[2,512]{1,0:T(2,128)S(1)}, f32[2,512,2048]{2,1,0:T(8,128)}) fusion(pred[512,2048]{1,0:T(8,128)(4,1)S(1)} %compare_and_fusion.2, bf16[512,2,128]{0,2,1:T(8,128)(2,1)S(1)} %bitcast.85, bf16[2048,2,128]{2,0,1:T(8,128)(2,1)} %get-tuple-element.207), kind=kOutput, calls=%fused_computation.48.clone.1 | convolution fusion | flops 545261568 | bytes 10752000 | tf_op jit(solution)/shard_map/while/body/eval_jaxpr/sub | solution.py:62
  199.4 5.2 %fusion.55 = bf16[2,512,128]{1,2,0:T(8,128)(2,1)S(1)} fusion(bf16[2048,2,128]{0,2,1:T(8,128)(2,1)} %get-tuple-element.208, f32[2,512,2048]{2,1,0:T(8,128)} %get-tuple-element.175, f32[2,512]{1,0:T(2,128)S(1)} %get-tuple-element.176), kind=kOutput, calls=%fused_computation.10.clone.1 | convolution fusion | flops 541196288 | bytes 9703424 | tf_op jit(solution)/shard_map/while/body/eval_jaxpr/hqk,khd->qhd/dot_general | solution.py:64
  206.2 0.9 compare_and_fusion.2
  207.2 7.8 %fusion.54 = (f32[2,512]{1,0:T(2,128)S(1)}, f32[2,512,2048]{2,1,0:T(8,128)}) fusion(pred[512,2048]{1,0:T(8,128)(4,1)S(1)} %compare_and_fusion.2, bf16[512,2,128]{0,2,1:T(8,128)(2,1)S(1)} %bitcast.85, bf16[2048,2,128]{2,0,1:T(8,128)(2,1)} %get-tuple-element.207), kind=kOutput, calls=%fused_computation.48.clone.1 | convolution fusion | flops 545261568 | bytes 10752000 | tf_op jit(solution)/shard_map/while/body/eval_jaxpr/sub | solution.py:62
  215.0 5.2 %fusion.55 = bf16[2,512,128]{1,2,0:T(8,128)(2,1)S(1)} fusion(bf16[2048,2,128]{0,2,1:T(8,128)(2,1)} %get-tuple-element.208, f32[2,512,2048]{2,1,0:T(8,128)} %get-tuple-element.175, f32[2,512]{1,0:T(2,128)S(1)} %get-tuple-element.176), kind=kOutput, calls=%fused_computation.10.clone.1 | convolution fusion | flops 541196288 | bytes 9703424 | tf_op jit(solution)/shard_map/while/body/eval_jaxpr/hqk,khd->qhd/dot_general | solution.py:64
  221.8 0.9 compare_and_fusion.2
  222.7 7.8 %fusion.54 = (f32[2,512]{1,0:T(2,128)S(1)}, f32[2,512,2048]{2,1,0:T(8,128)}) fusion(pred[512,2048]{1,0:T(8,128)(4,1)S(1)} %compare_and_fusion.2, bf16[512,2,128]{0,2,1:T(8,128)(2,1)S(1)} %bitcast.85, bf16[2048,2,128]{2,0,1:T(8,128)(2,1)} %get-tuple-element.207), kind=kOutput, calls=%fused_computation.48.clone.1 | convolution fusion | flops 545261568 | bytes 10752000 | tf_op jit(solution)/shard_map/while/body/eval_jaxpr/sub | solution.py:62
  230.5 5.3 %fusion.55 = bf16[2,512,128]{1,2,0:T(8,128)(2,1)S(1)} fusion(bf16[2048,2,128]{0,2,1:T(8,128)(2,1)} %get-tuple-element.208, f32[2,512,2048]{2,1,0:T(8,128)} %get-tuple-element.175, f32[2,512]{1,0:T(2,128)S(1)} %get-tuple-element.176), kind=kOutput, calls=%fused_computation.10.clone.1 | convolution fusion | flops 541196288 | bytes 9703424 | tf_op jit(solution)/shard_map/while/body/eval_jaxpr/hqk,khd->qhd/dot_general | solution.py:64
  237.4 0.9 compare_and_fusion.2
  238.3 7.8 %fusion.54 = (f32[2,512]{1,0:T(2,128)S(1)}, f32[2,512,2048]{2,1,0:T(8,128)}) fusion(pred[512,2048]{1,0:T(8,128)(4,1)S(1)} %compare_and_fusion.2, bf16[512,2,128]{0,2,1:T(8,128)(2,1)S(1)} %bitcast.85, bf16[2048,2,128]{2,0,1:T(8,128)(2,1)} %get-tuple-element.207), kind=kOutput, calls=%fused_computation.48.clone.1 | convolution fusion | flops 545261568 | bytes 10752000 | tf_op jit(solution)/shard_map/while/body/eval_jaxpr/sub | solution.py:62
  246.2 5.2 %fusion.55 = bf16[2,512,128]{1,2,0:T(8,128)(2,1)S(1)} fusion(bf16[2048,2,128]{0,2,1:T(8,128)(2,1)} %get-tuple-element.208, f32[2,512,2048]{2,1,0:T(8,128)} %get-tuple-element.175, f32[2,512]{1,0:T(2,128)S(1)} %get-tuple-element.176), kind=kOutput, calls=%fused_computation.10.clone.1 | convolution fusion | flops 541196288 | bytes 9703424 | tf_op jit(solution)/shard_map/while/body/eval_jaxpr/hqk,khd->qhd/dot_general | solution.py:64
  251.6 2.2 stack.3
  253.8 5.0 %all-to-all-start = ((bf16[4,2048,256]{2,1,0:T(8,128)(2,1)}), bf16[4,2048,256]{2,1,0:T(8,128)(2,1)}, u32[]{:S(2)}, u32[]{:S(2)}) async-start(bf16[4,2048,256]{2,1,0:T(8,128)(2,1)} %stack.3), calls=%async_computation | async-start | bytes 8388608 | tf_op jit(solution)/shard_map/all_to_all | solution.py:15
  259.5 5.7 %select_bitcast_fusion.4 = (f32[1,1,2048,256]{3,2,1,0:T(8,128)}, f32[1,1,2048,256]{3,2,1,0:T(8,128)}, f32[1,1,2048,256]{3,2,1,0:T(8,128)}, f32[1,1,2048,256]{3,2,1,0:T(8,128)}) fusion(pred[]{:T(512)S(6)} %eq.31, bf16[4,2048,256]{2,1,0:T(8,128)(2,1)} %all-gather.4.cloned.1.call-done), kind=kLoop, calls=%fused_computation.34 | loop fusion | flops 4194304 | bytes 12582913 | tf_op jit(solution)/shard_map/jit(_where)/select_n | solution.py:143
  265.2 5.7 %select_bitcast_fusion = (f32[1,1,2048,256]{3,2,1,0:T(8,128)}, f32[1,1,2048,256]{3,2,1,0:T(8,128)}, f32[1,1,2048,256]{3,2,1,0:T(8,128)}, f32[1,1,2048,256]{3,2,1,0:T(8,128)}) fusion(bf16[4,2048,256]{2,1,0:T(8,128)(2,1)} %all-gather.6.cloned.1.call-done, pred[]{:T(512)S(6)} %eq.31), kind=kLoop, calls=%fused_computation.30 | loop fusion | flops 4194304 | bytes 12582913 | tf_op jit(solution)/shard_map/jit(_where)/select_n | solution.py:143
  270.9 35.3 %all-to-all-done = bf16[4,2048,256]{2,1,0:T(8,128)(2,1)} async-done(((bf16[4,2048,256]{2,1,0:T(8,128)(2,1)}), bf16[4,2048,256]{2,1,0:T(8,128)(2,1)}, u32[]{:S(2)}, u32[]{:S(2)}) %all-to-all-start) | async-done | bytes 4194336 | tf_op jit(solution)/shard_map/all_to_all | solution.py:15
  306.1 6.2 %fusion.33 = bf16[1,1,2048,512]{3,2,1,0:T(8,128)(2,1)} fusion(bf16[4,2048,256]{2,1,0:T(8,128)(2,1)} %all-to-all-done, pred[]{:T(512)S(6)} %eq.31, bf16[4,512,256]{2,1,0:T(8,128)(2,1)} %all-to-all-done.1), kind=kOutput, calls=%fused_computation.29 | convolution fusion | flops 2149580800 | bytes 7340033 | tf_op jit(solution)/shard_map/dot_general | solution.py:122
  (59 shorter events, 7.2 us)
Async XLA Ops:
  7.2 55.5 %copy-start.1 = (f32[1,256,256]{2,1,0:T(8,128)S(1)}, f32[1,256,256]{2,1,0:T(8,128)}, u32[]{:S(2)}) copy-start(f32[1,256,256]{2,1,0:T(8,128)} %param.20) | copy-start | bytes 786436
  7.2 55.6 %copy-start.2 = (f32[1,256,256]{2,1,0:T(8,128)S(1)}, f32[1,256,256]{2,1,0:T(8,128)}, u32[]{:S(2)}) copy-start(f32[1,256,256]{2,1,0:T(8,128)} %param.21) | copy-start | bytes 786436
  7.2 55.6 %copy-start.3 = (f32[1,256,256]{2,1,0:T(8,128)S(1)}, f32[1,256,256]{2,1,0:T(8,128)}, u32[]{:S(2)}) copy-start(f32[1,256,256]{2,1,0:T(8,128)} %param.22) | copy-start | bytes 786436
  7.2 55.6 %copy-start.4 = (f32[1,256,256]{2,1,0:T(8,128)S(1)}, f32[1,256,256]{2,1,0:T(8,128)}, u32[]{:S(2)}) copy-start(f32[1,256,256]{2,1,0:T(8,128)} %param.23) | copy-start | bytes 786436
  7.2 56.5 %copy-start.5 = (s32[1,2048]{1,0:T(1,128)S(1)}, s32[1,2048]{1,0:T(1,128)}, u32[]{:S(2)}) copy-start(s32[1,2048]{1,0:T(1,128)} %param.14) | copy-start | bytes 24580
  7.2 79.1 %all-gather.4.cloned.1.call-start = ((), (), s32[]{:S(2)}) async-start(), calls=%async_computation.2 | async-start | bytes 4718592 | tf_op jit(solution)/shard_map/all_gather | solution.py:25
  12.1 165.1 %all-gather.8.cloned.1.call-start = ((), (), s32[]{:S(2)}) async-start(), calls=%async_computation.4 | async-start | bytes 10485760 | tf_op jit(solution)/shard_map/all_gather | solution.py:112
  12.2 49.2 %collective-permute-start = (bf16[1,1,2048,512]{3,2,1,0:T(8,128)(2,1)}, bf16[1,1,2048,512]{3,2,1,0:T(8,128)(2,1)S(1)}, u32[]{:S(2)}, u32[]{:S(2)}) collective-permute-start(bf16[1,1,2048,512]{3,2,1,0:T(8,128)(2,1)} %param.15), channel_id=1, source_target_pairs={{0,4},{4,8},{8,12},{12,0},{1,5},{5,9},{9,13},{13,1},{2,6},{6,10},{... | collective-permute-start | bytes 6291464 | tf_op jit(solution)/shard_map/ppermute | solution.py:30
  61.3 1.3 copy-start
  62.7 202.5 %all-gather.6.cloned.1.call-start = ((), (), s32[]{:S(2)}) async-start(), calls=%async_computation.3 | async-start | bytes 4718592 | tf_op jit(solution)/shard_map/all_gather | solution.py:25
  90.1 161.5 %all-to-all-start.1 = ((bf16[4,512,256]{2,1,0:T(8,128)(2,1)}), bf16[4,512,256]{2,1,0:T(8,128)(2,1)}, u32[]{:S(2)}, u32[]{:S(2)}) async-start(bf16[4,512,256]{2,1,0:T(8,128)(2,1)} %bitcast.21), calls=%async_computation.1 | async-start | bytes 2097152 | tf_op jit(solution)/shard_map/all_to_all | solution.py:121
  253.8 52.3 %all-to-all-start = ((bf16[4,2048,256]{2,1,0:T(8,128)(2,1)}), bf16[4,2048,256]{2,1,0:T(8,128)(2,1)}, u32[]{:S(2)}, u32[]{:S(2)}) async-start(bf16[4,2048,256]{2,1,0:T(8,128)(2,1)} %stack.3), calls=%async_computation | async-start | bytes 8388608 | tf_op jit(solution)/shard_map/all_to_all | solution.py:15
Sparse Core Ops, SparseCore 0:
  12.2 74.0 all-gather.3
  88.5 88.5 all-gather.7
  180.1 67.4 all-gather.5
